TPU v7x, 256 devices: a whole 4x4x8 slice. The times are simulated.
256 devices in a mesh: rep: 8 (over x, core), slab: 16 (over y, z_lo), pix: 2 (over z_hi).
Axes of the slice: x: 4, y: 4, z: 8 (z_hi: 2, z_lo: 4; z = z_hi * 4 + z_lo), core: 2. Of those that a mesh axis runs over, the one named last changes fastest.
Arguments:
- projections: bfloat16 [64, 256, 512], P(('rep', 'pix'), 'slab'), may hold values from -6 to 6
- ctf_weight: bfloat16 [64, 256, 256], P(('rep', 'pix'), 'slab'), may hold values from 0.099609375 to 4
- orient: int32 [64], P(('rep', 'pix')), may hold values from 0 to 63
- angle_table: int32 [64, 4, 256], replicated, may hold values from 0 to 255, as said below
Outputs:
- density: float32 [256, 256, 512], P(('rep', 'pix'), 'slab')
Inputs may be any that keep to these rules, and one draw needn't show every extreme that they name: `angle_table`: for every entry and column, the lower indices lie between 3 and 253, and the fractions between 0 and 255.
All inputs are finite; a program needn't handle non-finite values.
Results may differ from a plain program's by a relative error of at most 0.0022.
Values may be sent and summed in bfloat16 or wider, within the bound.
A program may use at most 128 MiB of HBM per device.

v0:
```python
import jax
import jax.numpy as jnp
from jax import lax
from jax.sharding import PartitionSpec as P


def from_everyone(value, axis):
    length = lax.axis_size(axis)
    return lax.all_to_all(
        jnp.broadcast_to(value[None], (length, *value.shape)), axis, 0, 0, tiled=True
    )


def in_order(blocks, dim):
    lengths = list(blocks.shape[1:])
    lengths[dim] *= blocks.shape[0]
    return jnp.moveaxis(blocks, 0, dim).reshape(lengths)


def gather_directly(value, axis, dim):
    blocks = from_everyone(value, axis)
    return in_order(blocks, dim)


def in_one_piece(arrays, axis, dim, along):
    both = jnp.concatenate(arrays, axis=along)
    out, at, done = (gather_directly(both, axis, dim), 0, [])
    for a in arrays:
        done.append(lax.slice_in_dim(out, at, at + a.shape[along], axis=along))
        at += a.shape[along]
    return tuple(done)


def corner_weights(first_index, index_count, lower_index, fraction):
    indices = first_index + lax.iota(jnp.int32, index_count)
    lower_hit = (indices[:, None, None] == lower_index[None, :, :]).astype(jnp.float32)
    upper_hit = (indices[:, None, None] == lower_index[None, :, :] + 1).astype(jnp.float32)
    fraction_weight = fraction.astype(jnp.float32)[None, :, :] / 256.0
    return lower_hit * (1.0 - fraction_weight) + upper_hit * fraction_weight


def lookup(orient, angle_table):
    choose = (orient[:, None] == lax.iota(jnp.int32, angle_table.shape[0])[None, :]).astype(
        jnp.int32
    )
    return jnp.sum(choose[:, :, None, None] * angle_table[None], axis=1)


def spread(samples, geometry, count_x, first_z, count_z, block_rows):
    flat_samples = samples.reshape(samples.shape[0] * samples.shape[1], samples.shape[2])
    weights_third = corner_weights(first_z, count_z, geometry[:, 2], geometry[:, 3])
    block_count = count_x // block_rows

    def one_block(block_start):
        weights_first = corner_weights(block_start, block_rows, geometry[:, 0], geometry[:, 1])
        matrix = (weights_first[:, None, :, :] * weights_third[None, :, :, :]).astype(jnp.bfloat16)
        matrix = matrix.reshape(block_rows * count_z, flat_samples.shape[0])
        summed = jnp.dot(matrix, flat_samples, preferred_element_type=jnp.float32)
        return summed.reshape(block_rows, count_z, samples.shape[2])

    starts = block_rows * lax.iota(jnp.int32, block_count)
    blocks = lax.map(one_block, starts)
    return blocks.reshape(count_x, count_z, samples.shape[2])


def body(projections, ctf_weight, orient, angle_table):
    planes = projections.shape[1]
    columns = projections.shape[2] // 2
    owned_rows = columns // (lax.axis_size("rep") * lax.axis_size("pix"))
    first_plane = lax.axis_index("slab") * planes
    whole_proj, whole_ctf = in_one_piece((projections, ctf_weight), "slab", 1, 2)
    samples = jnp.concatenate([whole_proj, whole_ctf], axis=2)
    geometry = lookup(orient, angle_table)
    volume_block = lax.psum_scatter(
        spread(
            samples,
            geometry,
            lax.axis_size(("rep", "pix")) * owned_rows,
            first_plane,
            planes,
            owned_rows,
        ),
        ("rep", "pix"),
        scatter_dimension=0,
        tiled=True,
    )
    values = volume_block[:, :, : 2 * columns].reshape(owned_rows, planes, 2, columns)
    density = volume_block[:, :, None, 2 * columns :] + 1.0
    return (values / density).reshape(owned_rows, planes, 2 * columns)


def solution(mesh):
    placed = (
        P(("rep", "pix"), "slab", None),
        P(("rep", "pix"), "slab", None),
        P(("rep", "pix")),
        P(),
    )
    return jax.shard_map(
        body, mesh=mesh, in_specs=placed, out_specs=P(("rep", "pix"), "slab", None), check_vma=False
    )
```

profile of v0, /device:TPU:96, one launch (start us, length us, event | category | flops | bytes accessed | tf_op | source)
XLA Modules:
  0.0 287.8 jit_solution(8248314757741077527)
XLA Ops:
  7.4 1.4 broadcast_in_dim.6
  8.8 7.7 %all-to-all-start = ((bf16[16,4,16,768]{3,2,1,0:T(8,128)(2,1)}), bf16[16,4,16,768]{3,2,1,0:T(8,128)(2,1)S(1)}, u32[]{:S(2)}, u32[]{:S(2)}) async-start(bf16[16,4,16,768]{3,2,1,0:T(8,128)(2,1)} %broadcast_in_dim.6), calls=%async_computation | async-start | bytes 3145728 | tf_op jit(solution)/shard_map/all_to_all | solution.py:9
  16.6 1.0 copy.15
  18.6 33.3 %all-to-all-done = bf16[16,4,16,768]{3,2,1,0:T(8,128)(2,1)S(1)} async-done(((bf16[16,4,16,768]{3,2,1,0:T(8,128)(2,1)}), bf16[16,4,16,768]{3,2,1,0:T(8,128)(2,1)S(1)}, u32[]{:S(2)}, u32[]{:S(2)}) %all-to-all-start) | async-done | bytes 1572896 | tf_op jit(solution)/shard_map/all_to_all | solution.py:9
  52.0 49.6 %while.13 = (s32[]{:T(128)}, f32[16,16,16,768]{3,2,1,0:T(8,128)}, s32[16]{0:T(128)S(1)}, s32[4,4,256]{2,1,0:T(4,128)S(1)}, f32[1,4,256]{2,1,0:T(4,128)S(1)}, /*i...) while((s32[]{:T(128)}, f32[16,16,16,768]{3,2,1,0:T(8,128)}, ...), condition=%wide.region_2.3_spmd.clone, body=%wide.region_1.2_spmd.clone.sunk | while | flops 403344416 | bytes 2827077 | solution.py:62
  53.7 1.5 fusion.19
  56.8 1.5 fusion.19
  59.9 1.5 fusion.19
  62.9 1.5 fusion.19
  66.0 1.5 fusion.19
  69.1 1.5 fusion.19
  72.2 1.5 fusion.19
  75.3 1.5 fusion.19
  78.4 1.5 fusion.19
  81.5 1.5 fusion.19
  84.6 1.5 fusion.19
  87.7 1.6 fusion.19
  90.9 1.5 fusion.19
  94.0 1.5 fusion.19
  97.1 1.5 fusion.19
  100.2 1.5 fusion.19
  101.7 175.7 %reduce-scatter.2.cloned.1.call-done = f32[16,16,768]{2,1,0:T(8,128)} async-done(((f32[256,16,768]{2,1,0:T(8,128)}), f32[16,16,768]{2,1,0:T(8,128)}) %reduce-scatter.2.cloned.1.call-update) | async-done | bytes 786448 | tf_op jit(solution)/shard_map/reduce_scatter | solution.py:74
  277.4 1.0 slice_add_fusion
  279.0 1.9 slice_divide_fusion
  (177 shorter events, 27.4 us)
Async XLA Ops:
  8.8 43.1 %all-to-all-start = ((bf16[16,4,16,768]{3,2,1,0:T(8,128)(2,1)}), bf16[16,4,16,768]{3,2,1,0:T(8,128)(2,1)S(1)}, u32[]{:S(2)}, u32[]{:S(2)}) async-start(bf16[16,4,16,768]{3,2,1,0:T(8,128)(2,1)} %broadcast_in_dim.6), calls=%async_computation | async-start | bytes 3145728 | tf_op jit(solution)/shard_map/all_to_all | solution.py:9
  16.5 260.9 %reduce-scatter.2.cloned.1.call-start = ((), (), s32[]{:S(2)}) async-start(), calls=%async_computation.2 | async-start | bytes 13369344 | tf_op jit(solution)/shard_map/reduce_scatter | solution.py:74
Sparse Core Ops, SparseCore 0:
  101.8 175.5 reduce-scatter.1
where the time goes:
time: 291 us; the launch traced here: 288 us
  waiting for transfers between devices  209 us (72%)
  matrix products  23.7 us (8%)
  other arithmetic  18.6 us (6%)
  local copies, waits for them, and re-layouts  14 us (5%)
  between operations  13.5 us (5%)
  starting transfers between devices  7.78 us (3%)
    reduce_scatter x1, waiting for transfers between devices, body(): lax.psum_scatter(spread(samples, geometry, lax.axis_size(('rep', 'pix'))...  176 us
    all_to_all x1, waiting for transfers between devices, from_everyone(): lax.all_to_all(jnp.broadcast_to(value[None], (length, *value.shape)), axi...  33.3 us
    dot_general x16, matrix products, one_block(): summed = jnp.dot(matrix, flat_samples, preferred_element_type=jnp.float32)  23.7 us
    add x17, other arithmetic, corner_weights(): indices = first_index + lax.iota(jnp.int32, index_count)  11 us
    dynamic_slice x16, local copies, waits for them, and re-layouts, spread(): blocks = lax.map(one_block, starts)  10.5 us
    all_to_all x1, starting transfers between devices, from_everyone(): lax.all_to_all(jnp.broadcast_to(value[None], (length, *value.shape)), axi...  7.74 us
  transfers between devices with their start and end apart: 2, of which 2 were waited for; matrix products, arithmetic and copies ran while one was open for 1% of the time, Pallas kernels for 0%

commit v1 on v0

v1 whole, which is shorter than its diff:
```python
import jax
import jax.numpy as jnp
from jax import lax
from jax.experimental import pallas as pl
from jax.experimental.pallas import tpu as pltpu
from jax.sharding import PartitionSpec as P

MESH = pl.DeviceIdType.MESH
RING = 8
STEPS_R = 4
STEPS_L = 3


def slot_r(t):
    return 2 + 4 * (t - 1)


def slot_l(t):
    return 3 + 4 * (t - 1)


def slot_pr(t):
    return 4 + 4 * (t - 1) if t < 4 else 15


def slot_pl(t):
    return 5 + 4 * (t - 1)


def kernel(
    orient_ref, proj_ref, ctf_ref, table_ref, out_ref,
    piece, landed, gath, acc, outbuf, back,
    send1, recv1, send_r, recv_r, send_l, recv_l, send_p, recv_p, send2, recv2,
):
    rep = lax.axis_index("rep")
    slab = lax.axis_index("slab")
    pix = lax.axis_index("pix")
    xc, core = rep // 2, rep % 2
    yc, zl = slab // 4, slab % 4
    zpos = pix * 4 + zl
    me = xc * 4 + yc
    sub = core * 2 + pix

    def plane(q):
        return ((q // 4) * 2 + core, (q % 4) * 4 + zl, pix)

    def along_z(step):
        z = (zpos + step + RING) % RING
        return (rep, yc * 4 + z % 4, z // 4)

    right, left = along_z(1), along_z(-1)
    partner = (xc * 2 + 1 - core, slab, pix)

    barrier = pltpu.get_barrier_semaphore()

    def greet(k, carry):
        pl.semaphore_signal(
            barrier, inc=1, device_id=plane((me + k) % 16), device_id_type=MESH
        )
        return carry

    lax.fori_loop(1, 16, greet, 0)
    for peer in (right, left, partner):
        pl.semaphore_signal(barrier, inc=1, device_id=peer, device_id_type=MESH)

    samples = proj_ref[...].reshape(64, 512).astype(jnp.float32)
    weights = ctf_ref[...].reshape(64, 256).astype(jnp.float32)
    real, imag = samples[:, :256], samples[:, 256:]
    first = jnp.concatenate([real, weights], axis=0).T
    second = jnp.concatenate([imag, imag], axis=0).T

    column = lax.broadcasted_iota(jnp.int32, (256, 128), 0)
    lane = lax.broadcasted_iota(jnp.int32, (256, 128), 1)
    geometry = jnp.zeros((4, 128), jnp.float32)
    for n in range(4):
        row = table_ref[orient_ref[n]].astype(jnp.float32).astype(jnp.bfloat16)
        pick = (column == slab * 16 + lane % 16) & ((lane // 16) % 4 == n)
        geometry += jnp.dot(
            row, pick.astype(jnp.float32).astype(jnp.bfloat16), preferred_element_type=jnp.float32
        )
    fx, fz = geometry[1:2] / 256.0, geometry[3:4] / 256.0
    facts = jnp.concatenate(
        [
            geometry[0:1],
            geometry[2:3],
            (1.0 - fx) * (1.0 - fz),
            (1.0 - fx) * fz,
            fx * (1.0 - fz),
            fx * fz,
            jnp.zeros((10, 128), jnp.float32),
        ],
        axis=0,
    )
    low_half = lax.broadcasted_iota(jnp.int32, (16, 128), 1) < 64
    for q in range(16):
        piece[q, 0:16, :] = first[16 * q : 16 * q + 16].astype(jnp.bfloat16)
        piece[q, 16:32, :] = jnp.where(
            low_half, second[16 * q : 16 * q + 16], facts
        ).astype(jnp.bfloat16)

    acc[...] = jnp.zeros_like(acc)
    pl.semaphore_wait(barrier, 18)

    def across(src, dst, send, recv, k, into):
        to = (me + k) % 16
        return pltpu.make_async_remote_copy(
            src_ref=src.at[to], dst_ref=dst.at[into], send_sem=send.at[to], recv_sem=recv.at[into],
            device_id=plane(to), device_id_type=MESH,
        )

    def start_across(*refs):
        def go(k, carry):
            across(*refs, k, me).start()
            return carry

        lax.fori_loop(1, 16, go, 0)

    def land_across(*refs):
        def go(k, carry):
            across(*refs, k, (me - k + 16) % 16).wait_recv()
            return carry

        lax.fori_loop(1, 16, go, 0)

    def drain_across(*refs):
        def go(k, carry):
            across(*refs, k, me).wait_send()
            return carry

        lax.fori_loop(1, 16, go, 0)

    start_across(piece, landed, send1, recv1)
    landed[me] = piece[me]
    land_across(piece, landed, send1, recv1)

    half = lax.broadcasted_iota(jnp.int32, (32, 128), 1) < 64
    for j in range(8):
        a = landed[2 * j].astype(jnp.float32)
        b = landed[2 * j + 1].astype(jnp.float32)
        top = jnp.where(half, a, pltpu.roll(b, 64, 1)).astype(jnp.bfloat16)
        bottom = jnp.where(half, pltpu.roll(a, 64, 1), b).astype(jnp.bfloat16)
        at = pl.ds(128 * (j % 2), 128)
        gath[j // 2, 0:32, at] = top
        gath[j // 2, 32:64, at] = bottom

    def move(src, dst, send, recv, to):
        return pltpu.make_async_remote_copy(
            src_ref=gath.at[pl.ds(4 * src, 4)], dst_ref=gath.at[pl.ds(4 * dst, 4)],
            send_sem=send, recv_sem=recv, device_id=to, device_id_type=MESH,
        )

    to_r = [move(0 if t == 1 else slot_r(t - 1), slot_r(t), send_r.at[t - 1], recv_r.at[t - 1], right)
            for t in range(1, 5)]
    to_l = [move(0 if t == 1 else slot_l(t - 1), slot_l(t), send_l.at[t - 1], recv_l.at[t - 1], left)
            for t in range(1, 4)]
    to_p = {0: move(0, 1, send_p.at[0], recv_p.at[0], partner)}
    for t in range(1, 5):
        to_p["r", t] = move(slot_r(t), slot_pr(t), send_p.at[2 * t - 1], recv_p.at[2 * t - 1], partner)
    for t in range(1, 4):
        to_p["l", t] = move(slot_l(t), slot_pl(t), send_p.at[2 * t], recv_p.at[2 * t], partner)

    row16 = lax.broadcasted_iota(jnp.int32, (16, 256), 0).astype(jnp.float32)

    def chunk(g, carry):
        block = gath[g]
        facts = block[48:64].astype(jnp.float32)
        x0 = facts[0:1].astype(jnp.int32)
        z0 = facts[1:2].astype(jnp.int32)

        def spread(v):
            return jnp.broadcast_to(v, (16, 256)).astype(jnp.bfloat16)

        total = None
        for i in range(2):
            xr = x0 + i
            x_ok = ((xr >> 4) & 3) == sub
            x_low = spread((xr & 15).astype(jnp.float32))
            keys, shares = [], []
            for j in range(2):
                zr = z0 + j
                ok = x_ok & (((zr >> 4) & 3) == zl)
                key = jnp.where(ok, (xr >> 6) * 64 + (zr >> 6) * 16 + (zr & 15), -1)
                keys.append(spread(key.astype(jnp.float32)))
                shares.append(spread(facts[2 + 2 * i + j : 3 + 2 * i + j]))
            zero = jnp.zeros((16, 256), jnp.bfloat16)
            right_side = []
            for t in range(16):
                here = (row16 + 16.0 * t).astype(jnp.bfloat16)
                right_side.append(
                    jnp.where(keys[0] == here, shares[0], jnp.where(keys[1] == here, shares[1], zero))
                )
            right_side = jnp.concatenate(right_side, axis=0)
            left_side = []
            for v in range(16):
                hit = x_low == jnp.full((16, 256), v, jnp.bfloat16)
                for c in range(3):
                    left_side.append(jnp.where(hit, block[16 * c : 16 * c + 16], zero))
            left_side = jnp.concatenate(left_side, axis=0)
            part = lax.dot_general(
                left_side, right_side, (((1,), (1,)), ((), ())), preferred_element_type=jnp.float32
            )
            total = part if total is None else total + part
        acc[...] += total
        return carry

    def compute(first_slot, count):
        lax.fori_loop(4 * first_slot, 4 * (first_slot + count), chunk, 0)

    to_r[0].start()
    to_l[0].start()
    to_p[0].start()
    compute(0, 1)
    for t in range(1, 5):
        to_r[t - 1].wait_recv()
        if t < 4:
            to_r[t].start()
        to_p["r", t].start()
        if t < 4:
            to_l[t - 1].wait_recv()
            if t < 3:
                to_l[t].start()
            to_p["l", t].start()
        if t == 1:
            to_p[0].wait_recv()
            compute(1, 3)
        else:
            to_p["r", t - 1].wait_recv()
            to_p["l", t - 1].wait_recv()
            compute(slot_pr(t - 1), 4 if t < 4 else 3)
    to_p["r", 4].wait_recv()
    compute(15, 1)

    rows = []
    for v in range(16):
        base = 48 * v
        bottom = acc[pl.ds(base + 32, 16), :] + 1.0
        rows.append(acc[pl.ds(base, 16), :] / bottom)
        rows.append(acc[pl.ds(base + 16, 16), :] / bottom)
    for m in range(4):
        turned = jnp.concatenate(rows[8 * m : 8 * m + 8], axis=0).T
        for o in range(16):
            outbuf[o, :, pl.ds(128 * m, 128)] = turned[16 * o : 16 * o + 16].astype(jnp.bfloat16)

    start_across(outbuf, back, send2, recv2)
    back[me] = outbuf[me]
    land_across(outbuf, back, send2, recv2)

    lanes = lax.broadcasted_iota(jnp.int32, (16, 128), 1) // 16
    for m in range(4):
        for high in range(2):
            tiles = [back[8 * high + k, :, pl.ds(128 * m, 128)].astype(jnp.float32) for k in range(8)]
            for bit in (1, 2, 4):
                clear = (lanes & bit) == 0
                fresh = list(tiles)
                for k in range(8):
                    if k & bit == 0:
                        a, b = tiles[k], tiles[k | bit]
                        fresh[k] = jnp.where(clear, a, pltpu.roll(b, 16 * bit, 1))
                        fresh[k | bit] = jnp.where(clear, pltpu.roll(a, 128 - 16 * bit, 1), b)
                tiles = fresh
            for k in range(8):
                v, part = 4 * m + k // 2, k % 2
                out_ref[v, :, pl.ds(256 * part + 128 * high, 128)] = tiles[k]

    drain_across(piece, landed, send1, recv1)
    for copy in to_r + to_l + list(to_p.values()):
        copy.wait_send()
    drain_across(outbuf, back, send2, recv2)


def body(projections, ctf_weight, orient, angle_table):
    dma = pltpu.SemaphoreType.DMA
    return pl.pallas_call(
        kernel,
        out_shape=jax.ShapeDtypeStruct((16, 16, 512), jnp.float32),
        in_specs=[
            pl.BlockSpec(memory_space=pltpu.SMEM),
            pl.BlockSpec(memory_space=pltpu.VMEM),
            pl.BlockSpec(memory_space=pltpu.VMEM),
            pl.BlockSpec(memory_space=pltpu.VMEM),
        ],
        out_specs=pl.BlockSpec(memory_space=pltpu.VMEM),
        scratch_shapes=[
            pltpu.VMEM((16, 32, 128), jnp.bfloat16),
            pltpu.VMEM((16, 32, 128), jnp.bfloat16),
            pltpu.VMEM((64, 64, 256), jnp.bfloat16),
            pltpu.VMEM((768, 256), jnp.float32),
            pltpu.VMEM((16, 16, 512), jnp.bfloat16),
            pltpu.VMEM((16, 16, 512), jnp.bfloat16),
            dma((16,)), dma((16,)),
            dma((4,)), dma((4,)), dma((3,)), dma((3,)), dma((8,)), dma((8,)),
            dma((16,)), dma((16,)),
        ],
        compiler_params=pltpu.CompilerParams(
            collective_id=0, has_side_effects=True, vmem_limit_bytes=48 * 1024 * 1024
        ),
    )(orient, projections, ctf_weight, angle_table)


def solution(mesh):
    placed = (
        P(("rep", "pix"), "slab", None),
        P(("rep", "pix"), "slab", None),
        P(("rep", "pix")),
        P(),
    )
    return jax.shard_map(
        body, mesh=mesh, in_specs=placed, out_specs=P(("rep", "pix"), "slab", None), check_vma=False
    )
```

time: 291 us -> 57 us (0.20)
  the two profiles are of different devices: /device:TPU:96 before, /device:TPU:8 now
where the time goes in v1:
time: 57 us; the launch traced here: 56.8 us
  Pallas kernels  52.8 us (93%)
  local copies, waits for them, and re-layouts  4 us (7%)
    pallas_call x1, Pallas kernels, body(): pl.pallas_call(kernel, out_shape=jax.ShapeDtypeStruct((16, 16, 512), jnp....  52.8 us
    unnamed x9, local copies, waits for them, and re-layouts  4 us

profile of v1, /device:TPU:8, one launch (start us, length us, event | category | flops | bytes accessed | tf_op | source)
XLA Modules:
  0.0 56.8 jit_solution(10120744089573828681)
XLA Ops:
  0.0 0.0 copy-start
  0.0 0.9 %copy-done = s32[64,4,256]{2,1,0:T(4,128)S(1)} copy-done((s32[64,4,256]{2,1,0:T(4,128)S(1)}, s32[64,4,256]{2,1,0:T(4,128)}, u32[]{:S(2)}) %copy-start) | copy-done | bytes 262168
  1.0 0.0 copy-start.1
  1.0 0.8 %copy-done.1 = bf16[4,16,512]{2,1,0:T(8,128)(2,1)S(1)} copy-done((bf16[4,16,512]{2,1,0:T(8,128)(2,1)S(1)}, bf16[4,16,512]{2,1,0:T(8,128)(2,1)}, u32[]{:S(2)}) %copy-start.1) | copy-done | bytes 65560
  1.8 0.0 copy-start.2
  1.8 0.8 %copy-done.2 = bf16[4,16,256]{2,1,0:T(8,128)(2,1)S(1)} copy-done((bf16[4,16,256]{2,1,0:T(8,128)(2,1)S(1)}, bf16[4,16,256]{2,1,0:T(8,128)(2,1)}, u32[]{:S(2)}) %copy-start.2) | copy-done | bytes 32792
  2.5 0.0 copy-start.3
  2.6 0.7 %copy-done.3 = s32[4]{0:T(128)S(1)} copy-done((s32[4]{0:T(128)S(1)}, s32[4]{0:T(128)}, u32[]{:S(2)}) %copy-start.3) | copy-done | bytes 40
  3.2 52.8 %shard_map.46 = f32[16,16,512]{2,1,0:T(8,128)S(1)} custom-call(s32[4]{0:T(128)S(1)} %copy-done.3, bf16[4,16,512]{2,1,0:T(8,128)(2,1)S(1)} %copy-done.1, bf16[4,16,256]{2,1,0:T(8,128)(2,1)S(1)} %copy-done.2, s32[64,4,256]{2,1,0:T(4,128)S(1)} %copy-done), custom_call_target="tpu_custom_call" | custom-call | tf_op jit(solution)/shard_map/pallas_call | solution.py:273
  56.0 0.8 %copy.6 = f32[16,16,512]{2,1,0:T(8,128)} copy(f32[16,16,512]{2,1,0:T(8,128)S(1)} %shard_map.46) | data formatting | bytes 1048576
Async XLA Ops:
  0.0 0.9 %copy-start = (s32[64,4,256]{2,1,0:T(4,128)S(1)}, s32[64,4,256]{2,1,0:T(4,128)}, u32[]{:S(2)}) copy-start(s32[64,4,256]{2,1,0:T(4,128)} %table_ref.1) | copy-start | bytes 786436
  1.0 0.8 %copy-start.1 = (bf16[4,16,512]{2,1,0:T(8,128)(2,1)S(1)}, bf16[4,16,512]{2,1,0:T(8,128)(2,1)}, u32[]{:S(2)}) copy-start(bf16[4,16,512]{2,1,0:T(8,128)(2,1)} %proj_ref.1) | copy-start | bytes 196612
  1.8 0.8 %copy-start.2 = (bf16[4,16,256]{2,1,0:T(8,128)(2,1)S(1)}, bf16[4,16,256]{2,1,0:T(8,128)(2,1)}, u32[]{:S(2)}) copy-start(bf16[4,16,256]{2,1,0:T(8,128)(2,1)} %ctf_ref.1) | copy-start | bytes 98308
  2.5 0.7 %copy-start.3 = (s32[4]{0:T(128)S(1)}, s32[4]{0:T(128)}, u32[]{:S(2)}) copy-start(s32[4]{0:T(128)} %orient_ref.1) | copy-start | bytes 52

commit v2 on v1

--- a/solution.py
+++ b/solution.py
@@ -7,8 +7,7 @@
 
 MESH = pl.DeviceIdType.MESH
 RING = 8
-STEPS_R = 4
-STEPS_L = 3
+FAR = 14
 
 
 def slot_r(t):
@@ -20,7 +19,7 @@
 
 
 def slot_pr(t):
-    return 4 + 4 * (t - 1) if t < 4 else 15
+    return 4 + 4 * (t - 1)
 
 
 def slot_pl(t):
@@ -28,10 +27,18 @@
 
 
 def kernel(
-    orient_ref, proj_ref, ctf_ref, table_ref, out_ref,
-    piece, landed, gath, acc, outbuf, back,
+    orient_hbm, proj_hbm, ctf_hbm, table_hbm, out_ref,
+    orient_ref, proj_ref, ctf_ref, table_ref, stage, piece, landed, gath, acc, outbuf, back,
     send1, recv1, send_r, recv_r, send_l, recv_l, send_p, recv_p, send2, recv2,
 ):
+    staged = [
+        pltpu.make_async_copy(src, dst, stage.at[k])
+        for k, (src, dst) in enumerate(
+            ((orient_hbm, orient_ref), (proj_hbm, proj_ref), (ctf_hbm, ctf_ref), (table_hbm, table_ref))
+        )
+    ]
+    for copy in staged:
+        copy.start()
     rep = lax.axis_index("rep")
     slab = lax.axis_index("slab")
     pix = lax.axis_index("pix")
@@ -62,6 +69,10 @@
     lax.fori_loop(1, 16, greet, 0)
     for peer in (right, left, partner):
         pl.semaphore_signal(barrier, inc=1, device_id=peer, device_id_type=MESH)
+
+    acc[...] = jnp.zeros_like(acc)
+    for copy in staged:
+        copy.wait()
 
     samples = proj_ref[...].reshape(64, 512).astype(jnp.float32)
     weights = ctf_ref[...].reshape(64, 256).astype(jnp.float32)
@@ -98,7 +109,6 @@
             low_half, second[16 * q : 16 * q + 16], facts
         ).astype(jnp.bfloat16)
 
-    acc[...] = jnp.zeros_like(acc)
     pl.semaphore_wait(barrier, 18)
 
     def across(src, dst, send, recv, k, into):
@@ -143,25 +153,48 @@
         gath[j // 2, 0:32, at] = top
         gath[j // 2, 32:64, at] = bottom
 
-    def move(src, dst, send, recv, to):
+    def move(src, dst, part, send, recv, to):
         return pltpu.make_async_remote_copy(
-            src_ref=gath.at[pl.ds(4 * src, 4)], dst_ref=gath.at[pl.ds(4 * dst, 4)],
+            src_ref=gath.at[pl.ds(4 * src + 2 * part, 2)], dst_ref=gath.at[pl.ds(4 * dst + 2 * part, 2)],
             send_sem=send, recv_sem=recv, device_id=to, device_id_type=MESH,
         )
 
-    to_r = [move(0 if t == 1 else slot_r(t - 1), slot_r(t), send_r.at[t - 1], recv_r.at[t - 1], right)
-            for t in range(1, 5)]
-    to_l = [move(0 if t == 1 else slot_l(t - 1), slot_l(t), send_l.at[t - 1], recv_l.at[t - 1], left)
-            for t in range(1, 4)]
-    to_p = {0: move(0, 1, send_p.at[0], recv_p.at[0], partner)}
-    for t in range(1, 5):
-        to_p["r", t] = move(slot_r(t), slot_pr(t), send_p.at[2 * t - 1], recv_p.at[2 * t - 1], partner)
-    for t in range(1, 4):
-        to_p["l", t] = move(slot_l(t), slot_pl(t), send_p.at[2 * t], recv_p.at[2 * t], partner)
+    def ringed(side, t, part):
+        slot, send, recv, to = (
+            (slot_r, send_r, recv_r, right) if side == "r" else (slot_l, send_l, recv_l, left)
+        )
+        src = 0 if t == 1 else slot(t - 1)
+        k = 2 * (t - 1) + part
+        return move(src, FAR if t == 4 else slot(t), part, send.at[k], recv.at[k], to)
+
+    def shared(side, t, part):
+        if t == 0:
+            src, dst, k = 0, 1, 0
+        elif t == 4:
+            src, dst, k = FAR, FAR + 1, 7
+        else:
+            src, dst = (slot_r(t), slot_pr(t)) if side == "r" else (slot_l(t), slot_pl(t))
+            k = 2 * t - (1 if side == "r" else 0)
+        return move(src, dst, part, send_p.at[2 * k + part], recv_p.at[2 * k + part], partner)
+
+    started = []
+
+    def start(copy):
+        copy.start()
+        started.append(copy)
+
+    def arrive(t, part):
+        for side in ("r", "l"):
+            if t == 4 and part != (0 if side == "r" else 1):
+                continue
+            ringed(side, t, part).wait_recv()
+            if t < 3 or (t == 3 and part == (0 if side == "r" else 1)):
+                start(ringed(side, t + 1, part))
+            start(shared(side, t, part))
 
     row16 = lax.broadcasted_iota(jnp.int32, (16, 256), 0).astype(jnp.float32)
 
-    def chunk(g, carry):
+    def operands(g):
         block = gath[g]
         facts = block[48:64].astype(jnp.float32)
         x0 = facts[0:1].astype(jnp.int32)
@@ -170,7 +203,8 @@
         def spread(v):
             return jnp.broadcast_to(v, (16, 256)).astype(jnp.bfloat16)
 
-        total = None
+        zero = jnp.zeros((16, 256), jnp.bfloat16)
+        pairs = []
         for i in range(2):
             xr = x0 + i
             x_ok = ((xr >> 4) & 3) == sub
@@ -182,53 +216,67 @@
                 key = jnp.where(ok, (xr >> 6) * 64 + (zr >> 6) * 16 + (zr & 15), -1)
                 keys.append(spread(key.astype(jnp.float32)))
                 shares.append(spread(facts[2 + 2 * i + j : 3 + 2 * i + j]))
-            zero = jnp.zeros((16, 256), jnp.bfloat16)
             right_side = []
             for t in range(16):
                 here = (row16 + 16.0 * t).astype(jnp.bfloat16)
                 right_side.append(
                     jnp.where(keys[0] == here, shares[0], jnp.where(keys[1] == here, shares[1], zero))
                 )
-            right_side = jnp.concatenate(right_side, axis=0)
             left_side = []
             for v in range(16):
                 hit = x_low == jnp.full((16, 256), v, jnp.bfloat16)
                 for c in range(3):
                     left_side.append(jnp.where(hit, block[16 * c : 16 * c + 16], zero))
-            left_side = jnp.concatenate(left_side, axis=0)
-            part = lax.dot_general(
-                left_side, right_side, (((1,), (1,)), ((), ())), preferred_element_type=jnp.float32
-            )
-            total = part if total is None else total + part
-        acc[...] += total
+            pairs.append((left_side, jnp.concatenate(right_side, axis=0)))
+        return pairs
+
+    def nt(a, b):
+        return lax.dot_general(a, b, (((1,), (1,)), ((), ())), preferred_element_type=jnp.float32)
+
+    def block_step(b, carry):
+        pairs = []
+        for e in range(4):
+            pairs += operands(4 * b + e)
+        size = 48 // 2
+        for h in range(2):
+            total = None
+            for left_side, right_side in pairs:
+                part = nt(jnp.concatenate(left_side[size * h : size * h + size], axis=0), right_side)
+                total = part if total is None else total + part
+            acc[pl.ds(16 * size * h, 16 * size), :] += total
         return carry
 
     def compute(first_slot, count):
-        lax.fori_loop(4 * first_slot, 4 * (first_slot + count), chunk, 0)
-
-    to_r[0].start()
-    to_l[0].start()
-    to_p[0].start()
+        lax.fori_loop(first_slot, first_slot + count, block_step, 0)
+
+    for part in range(2):
+        start(ringed("r", 1, part))
+        start(ringed("l", 1, part))
+        start(shared("r", 0, part))
     compute(0, 1)
-    for t in range(1, 5):
-        to_r[t - 1].wait_recv()
-        if t < 4:
-            to_r[t].start()
-        to_p["r", t].start()
-        if t < 4:
-            to_l[t - 1].wait_recv()
-            if t < 3:
-                to_l[t].start()
-            to_p["l", t].start()
-        if t == 1:
-            to_p[0].wait_recv()
-            compute(1, 3)
-        else:
-            to_p["r", t - 1].wait_recv()
-            to_p["l", t - 1].wait_recv()
-            compute(slot_pr(t - 1), 4 if t < 4 else 3)
-    to_p["r", 4].wait_recv()
-    compute(15, 1)
+    for part in range(2):
+        shared("r", 0, part).wait_recv()
+    compute(1, 1)
+
+    def shared_block(t):
+        for part in range(2):
+            shared("r", t, part).wait_recv()
+            shared("l", t, part).wait_recv()
+        compute(slot_pr(t), 2)
+
+    for t in range(1, 4):
+        arrive(t, 0)
+        if t > 1:
+            shared_block(t - 1)
+        arrive(t, 1)
+        compute(slot_r(t), 2)
+    arrive(4, 0)
+    shared_block(3)
+    arrive(4, 1)
+    compute(FAR, 1)
+    for part in range(2):
+        shared("r", 4, part).wait_recv()
+    compute(FAR + 1, 1)
 
     rows = []
     for v in range(16):
@@ -263,7 +311,7 @@
                 out_ref[v, :, pl.ds(256 * part + 128 * high, 128)] = tiles[k]
 
     drain_across(piece, landed, send1, recv1)
-    for copy in to_r + to_l + list(to_p.values()):
+    for copy in started:
         copy.wait_send()
     drain_across(outbuf, back, send2, recv2)
 
@@ -273,14 +321,14 @@
     return pl.pallas_call(
         kernel,
         out_shape=jax.ShapeDtypeStruct((16, 16, 512), jnp.float32),
-        in_specs=[
-            pl.BlockSpec(memory_space=pltpu.SMEM),
-            pl.BlockSpec(memory_space=pltpu.VMEM),
-            pl.BlockSpec(memory_space=pltpu.VMEM),
-            pl.BlockSpec(memory_space=pltpu.VMEM),
-        ],
+        in_specs=[pl.BlockSpec(memory_space=pltpu.HBM)] * 4,
         out_specs=pl.BlockSpec(memory_space=pltpu.VMEM),
         scratch_shapes=[
+            pltpu.SMEM((4,), jnp.int32),
+            pltpu.VMEM((4, 16, 512), jnp.bfloat16),
+            pltpu.VMEM((4, 16, 256), jnp.bfloat16),
+            pltpu.VMEM((64, 4, 256), jnp.int32),
+            dma((4,)),
             pltpu.VMEM((16, 32, 128), jnp.bfloat16),
             pltpu.VMEM((16, 32, 128), jnp.bfloat16),
             pltpu.VMEM((64, 64, 256), jnp.bfloat16),
@@ -288,7 +336,7 @@
             pltpu.VMEM((16, 16, 512), jnp.bfloat16),
             pltpu.VMEM((16, 16, 512), jnp.bfloat16),
             dma((16,)), dma((16,)),
-            dma((4,)), dma((4,)), dma((3,)), dma((3,)), dma((8,)), dma((8,)),
+            dma((8,)), dma((8,)), dma((8,)), dma((8,)), dma((16,)), dma((16,)),
             dma((16,)), dma((16,)),
         ],
         compiler_params=pltpu.CompilerParams(

time: 57 us -> 48.3 us (0.85)
  the two profiles are of different devices: /device:TPU:8 before, /device:TPU:1 now
where the time goes in v2:
time: 48.3 us; the launch traced here: 48.1 us
  Pallas kernels  44 us (91%)
  local copies, waits for them, and re-layouts  4 us (8%)
    pallas_call x1, Pallas kernels, body(): pl.pallas_call(kernel, out_shape=jax.ShapeDtypeStruct((16, 16, 512), jnp....  44 us
    unnamed x9, local copies, waits for them, and re-layouts  4 us

profile of v2, /device:TPU:1, one launch (start us, length us, event | category | flops | bytes accessed | tf_op | source)
XLA Modules:
  0.0 48.1 jit_solution(10861612510726554067)
XLA Ops:
  0.0 0.0 copy-start
  0.0 0.9 %copy-done = s32[64,4,256]{2,1,0:T(4,128)S(1)} copy-done((s32[64,4,256]{2,1,0:T(4,128)S(1)}, s32[64,4,256]{2,1,0:T(4,128)}, u32[]{:S(2)}) %copy-start) | copy-done | bytes 262168
  1.0 0.0 copy-start.1
  1.0 0.8 %copy-done.1 = bf16[4,16,512]{2,1,0:T(8,128)(2,1)S(1)} copy-done((bf16[4,16,512]{2,1,0:T(8,128)(2,1)S(1)}, bf16[4,16,512]{2,1,0:T(8,128)(2,1)}, u32[]{:S(2)}) %copy-start.1) | copy-done | bytes 65560
  1.8 0.0 copy-start.2
  1.8 0.8 %copy-done.2 = bf16[4,16,256]{2,1,0:T(8,128)(2,1)S(1)} copy-done((bf16[4,16,256]{2,1,0:T(8,128)(2,1)S(1)}, bf16[4,16,256]{2,1,0:T(8,128)(2,1)}, u32[]{:S(2)}) %copy-start.2) | copy-done | bytes 32792
  2.5 0.0 copy-start.3
  2.6 0.7 %copy-done.3 = s32[4]{0:T(128)S(1)} copy-done((s32[4]{0:T(128)S(1)}, s32[4]{0:T(128)}, u32[]{:S(2)}) %copy-start.3) | copy-done | bytes 40
  3.2 44.0 %shard_map.46 = f32[16,16,512]{2,1,0:T(8,128)S(1)} custom-call(s32[4]{0:T(128)S(1)} %copy-done.3, bf16[4,16,512]{2,1,0:T(8,128)(2,1)S(1)} %copy-done.1, bf16[4,16,256]{2,1,0:T(8,128)(2,1)S(1)} %copy-done.2, s32[64,4,256]{2,1,0:T(4,128)S(1)} %copy-done), custom_call_target="tpu_custom_call" | custom-call | tf_op jit(solution)/shard_map/pallas_call | solution.py:321
  47.3 0.8 %copy.6 = f32[16,16,512]{2,1,0:T(8,128)} copy(f32[16,16,512]{2,1,0:T(8,128)S(1)} %shard_map.46) | data formatting | bytes 1048576
Async XLA Ops:
  0.0 0.9 %copy-start = (s32[64,4,256]{2,1,0:T(4,128)S(1)}, s32[64,4,256]{2,1,0:T(4,128)}, u32[]{:S(2)}) copy-start(s32[64,4,256]{2,1,0:T(4,128)} %table_hbm.1) | copy-start | bytes 786436
  1.0 0.8 %copy-start.1 = (bf16[4,16,512]{2,1,0:T(8,128)(2,1)S(1)}, bf16[4,16,512]{2,1,0:T(8,128)(2,1)}, u32[]{:S(2)}) copy-start(bf16[4,16,512]{2,1,0:T(8,128)(2,1)} %proj_hbm.1) | copy-start | bytes 196612
  1.8 0.8 %copy-start.2 = (bf16[4,16,256]{2,1,0:T(8,128)(2,1)S(1)}, bf16[4,16,256]{2,1,0:T(8,128)(2,1)}, u32[]{:S(2)}) copy-start(bf16[4,16,256]{2,1,0:T(8,128)(2,1)} %ctf_hbm.1) | copy-start | bytes 98308
  2.5 0.7 %copy-start.3 = (s32[4]{0:T(128)S(1)}, s32[4]{0:T(128)}, u32[]{:S(2)}) copy-start(s32[4]{0:T(128)} %orient_hbm.1) | copy-start | bytes 52

commit v3 on v2

v3 whole, which is shorter than its diff:
```python
import jax
import jax.numpy as jnp
from jax import lax
from jax.experimental import pallas as pl
from jax.experimental.pallas import tpu as pltpu
from jax.sharding import PartitionSpec as P

MESH = pl.DeviceIdType.MESH
RING = 8
FAR = 14
HALVES = ((0, 112), (112, 96))


def slot_of(side, t):
    return 2 + 4 * (t - 1) + side


def slot_shared(side, t):
    return 4 + 4 * (t - 1) + side


def kernel(
    orient_hbm, proj_hbm, ctf_hbm, table_hbm, out_ref,
    orient_ref, proj_ref, ctf_ref, table_ref, stage, piece, landed, gath, acc, outbuf, back,
    send1, recv1, send_z, recv_z, send_p, recv_p, send2, recv2,
):
    staged = [
        pltpu.make_async_copy(src, dst, stage.at[k])
        for k, (src, dst) in enumerate(
            ((orient_hbm, orient_ref), (proj_hbm, proj_ref), (ctf_hbm, ctf_ref), (table_hbm, table_ref))
        )
    ]
    for copy in staged:
        copy.start()
    rep = lax.axis_index("rep")
    slab = lax.axis_index("slab")
    pix = lax.axis_index("pix")
    xc, core = rep // 2, rep % 2
    yc, zl = slab // 4, slab % 4
    zpos = pix * 4 + zl
    me = xc * 4 + yc
    sub = core * 2 + pix

    def plane(q):
        return ((q // 4) * 2 + core, (q % 4) * 4 + zl, pix)

    def along_z(step):
        z = (zpos + step + RING) % RING
        return (rep, yc * 4 + z % 4, z // 4)

    partner = (xc * 2 + 1 - core, slab, pix)

    barrier = pltpu.get_barrier_semaphore()

    def greet(k, carry):
        pl.semaphore_signal(
            barrier, inc=1, device_id=plane((me + k) % 16), device_id_type=MESH
        )
        return carry

    lax.fori_loop(1, 16, greet, 0)
    for peer in (along_z(1), along_z(-1), along_z(2), along_z(-2), partner):
        pl.semaphore_signal(barrier, inc=1, device_id=peer, device_id_type=MESH)

    acc[...] = jnp.zeros_like(acc)
    for copy in staged:
        copy.wait()

    samples = proj_ref[...].reshape(64, 512).astype(jnp.float32)
    weights = ctf_ref[...].reshape(64, 256).astype(jnp.float32)
    real, imag = samples[:, :256], samples[:, 256:]
    first = jnp.concatenate([real, weights], axis=0).T
    second = jnp.concatenate([imag, imag], axis=0).T

    column = lax.broadcasted_iota(jnp.int32, (256, 128), 0)
    lane = lax.broadcasted_iota(jnp.int32, (256, 128), 1)
    geometry = jnp.zeros((4, 128), jnp.float32)
    for n in range(4):
        row = table_ref[orient_ref[n]].astype(jnp.float32).astype(jnp.bfloat16)
        pick = (column == slab * 16 + lane % 16) & ((lane // 16) % 4 == n)
        geometry += jnp.dot(
            row, pick.astype(jnp.float32).astype(jnp.bfloat16), preferred_element_type=jnp.float32
        )
    facts = jnp.concatenate(
        [
            geometry[0:1], geometry[2:3], geometry[1:2], geometry[3:4],
            jnp.zeros((12, 128), jnp.float32),
        ],
        axis=0,
    )
    low_half = lax.broadcasted_iota(jnp.int32, (16, 128), 1) < 64
    for q in range(16):
        piece[q, 0:16, :] = first[16 * q : 16 * q + 16].astype(jnp.bfloat16)
        piece[q, 16:32, :] = jnp.where(
            low_half, second[16 * q : 16 * q + 16], facts
        ).astype(jnp.bfloat16)

    pl.semaphore_wait(barrier, 20)

    def across(src, dst, send, recv, k, into):
        to = (me + k) % 16
        return pltpu.make_async_remote_copy(
            src_ref=src.at[to], dst_ref=dst.at[into], send_sem=send.at[to], recv_sem=recv.at[into],
            device_id=plane(to), device_id_type=MESH,
        )

    def start_across(*refs):
        def go(k, carry):
            across(*refs, k, me).start()
            return carry

        lax.fori_loop(1, 16, go, 0)

    def land_across(*refs):
        def go(k, carry):
            across(*refs, k, (me - k + 16) % 16).wait_recv()
            return carry

        lax.fori_loop(1, 16, go, 0)

    def drain_across(*refs):
        def go(k, carry):
            across(*refs, k, me).wait_send()
            return carry

        lax.fori_loop(1, 16, go, 0)

    start_across(piece, landed, send1, recv1)
    landed[me] = piece[me]
    land_across(piece, landed, send1, recv1)

    half = lax.broadcasted_iota(jnp.int32, (32, 128), 1) < 64
    tables = []
    for j in range(8):
        a = landed[2 * j].astype(jnp.float32)
        b = landed[2 * j + 1].astype(jnp.float32)
        top = jnp.where(half, a, pltpu.roll(b, 64, 1)).astype(jnp.bfloat16)
        bottom = jnp.where(half, pltpu.roll(a, 64, 1), b)
        at = pl.ds(128 * (j % 2), 128)
        row = 16 + 48 * (j // 2)
        gath[0, row : row + 32, at] = top
        gath[0, row + 32 : row + 48, at] = bottom[0:16].astype(jnp.bfloat16)
        tables.append(bottom[16:20])
    gath[0, 0:16, :] = jnp.concatenate(
        [
            jnp.concatenate([tables[2 * g][f : f + 1], tables[2 * g + 1][f : f + 1]], axis=1)
            for f in range(4)
            for g in range(4)
        ],
        axis=0,
    ).astype(jnp.bfloat16)

    def move(src, dst, rows, send, recv, to):
        at = pl.ds(rows[0], rows[1])
        return pltpu.make_async_remote_copy(
            src_ref=gath.at[src, at], dst_ref=gath.at[dst, at],
            send_sem=send, recv_sem=recv, device_id=to, device_id_type=MESH,
        )

    def ringed(side, t, part):
        src = 0 if t < 3 else slot_of(side, 2)
        dst = FAR if t == 4 else slot_of(side, t)
        k = 8 * side + 2 * (t - 1) + part
        reach = (1, 2, 1, 2)[t - 1]
        return move(
            src, dst, HALVES[part], send_z.at[k], recv_z.at[k], along_z(reach * (1 - 2 * side))
        )

    def shared(side, t, part):
        if t == 0:
            src, dst, k = 0, 1, 0
        elif t == 4:
            src, dst, k = FAR, FAR + 1, 7
        else:
            src, dst, k = slot_of(side, t), slot_shared(side, t), 2 * t - 1 + side
        k = 2 * k + part
        return move(src, dst, HALVES[part], send_p.at[k], recv_p.at[k], partner)

    def arrive(side, t):
        for part in range(2):
            ringed(side, t, part).wait_recv()
            if t == 2:
                ringed(side, 3, part).start()

                @pl.when(side == part)
                def _():
                    ringed(part, 4, part).start()

            shared(side, t, part).start()

    row16 = lax.broadcasted_iota(jnp.int32, (16, 256), 0).astype(jnp.float32)

    def operands(block, g, keys, lows, shares):
        def spread(v):
            return jnp.broadcast_to(v[g : g + 1], (16, 256)).astype(jnp.bfloat16)

        base = 16 + 48 * g
        zero = jnp.zeros((16, 256), jnp.bfloat16)
        pairs = []
        for i in range(2):
            x_low = spread(lows[i])
            key = [spread(keys[i][j]) for j in range(2)]
            share = [spread(shares[i][j]) for j in range(2)]
            right_side = []
            for t in range(16):
                here = (row16 + 16.0 * t).astype(jnp.bfloat16)
                right_side.append(
                    jnp.where(key[0] == here, share[0], jnp.where(key[1] == here, share[1], zero))
                )
            left_side = []
            for v in range(16):
                hit = x_low == jnp.full((16, 256), v, jnp.bfloat16)
                for c in range(3):
                    left_side.append(
                        jnp.where(hit, block[base + 16 * c : base + 16 * c + 16], zero)
                    )
            pairs.append((left_side, jnp.concatenate(right_side, axis=0)))
        return pairs

    def nt(a, b):
        return lax.dot_general(a, b, (((1,), (1,)), ((), ())), preferred_element_type=jnp.float32)

    def factors(slot):
        block = gath[slot]
        facts = block[0:16].astype(jnp.float32)
        x0, z0 = facts[0:4].astype(jnp.int32), facts[4:8].astype(jnp.int32)
        fx, fz = facts[8:12] / 256.0, facts[12:16] / 256.0
        keys, lows, shares = [], [], []
        for i in range(2):
            xr = x0 + i
            x_ok = ((xr >> 4) & 3) == sub
            lows.append((xr & 15).astype(jnp.float32))
            keys.append([])
            shares.append([])
            for j in range(2):
                zr = z0 + j
                ok = x_ok & (((zr >> 4) & 3) == zl)
                key = jnp.where(ok, (xr >> 6) * 64 + (zr >> 6) * 16 + (zr & 15), -1)
                keys[i].append(key.astype(jnp.float32))
                shares[i].append((fx if i else 1.0 - fx) * (fz if j else 1.0 - fz))
        pairs = []
        for g in range(4):
            pairs += operands(block, g, keys, lows, shares)
        return pairs

    def accumulate(*slots):
        pairs = []
        for slot in slots:
            pairs += factors(slot)
        for h in range(2):
            total = None
            for left_side, right_side in pairs:
                part = nt(jnp.concatenate(left_side[24 * h : 24 * h + 24], axis=0), right_side)
                total = part if total is None else total + part
            acc[pl.ds(384 * h, 384), :] += total

    near = jnp.where(zpos < 4, 1, 0)
    away = 1 - near

    for t in range(1, 3):
        for part in range(2):
            for side in range(2):
                ringed(side, t, part).start()
            if t == 1:
                shared(0, 0, part).start()

    def landed_shared(side, t):
        for part in range(2):
            shared(side, t, part).wait_recv()
        return {0: 1, 4: FAR + 1}[t] if t in (0, 4) else slot_shared(side, t)

    accumulate(0)
    accumulate(landed_shared(0, 0))
    arrive(near, 1)
    accumulate(slot_of(near, 1))
    arrive(away, 1)
    accumulate(landed_shared(near, 1), slot_of(away, 1))
    arrive(near, 2)
    accumulate(landed_shared(away, 1), slot_of(near, 2))
    arrive(away, 2)
    accumulate(landed_shared(near, 2), slot_of(away, 2))
    arrive(near, 3)
    accumulate(landed_shared(away, 2), slot_of(near, 3))
    arrive(away, 3)
    for side in range(2):
        ringed(side, 4, side).wait_recv()
        shared(0, 4, side).start()
    accumulate(landed_shared(near, 3), slot_of(away, 3))
    accumulate(landed_shared(away, 3), FAR)
    accumulate(landed_shared(0, 4))

    rows = []
    for v in range(16):
        base = 48 * v
        bottom = acc[pl.ds(base + 32, 16), :] + 1.0
        rows.append(acc[pl.ds(base, 16), :] / bottom)
        rows.append(acc[pl.ds(base + 16, 16), :] / bottom)
    for m in range(4):
        turned = jnp.concatenate(rows[8 * m : 8 * m + 8], axis=0).T
        for o in range(16):
            outbuf[o, :, pl.ds(128 * m, 128)] = turned[16 * o : 16 * o + 16].astype(jnp.bfloat16)

    start_across(outbuf, back, send2, recv2)
    back[me] = outbuf[me]
    land_across(outbuf, back, send2, recv2)

    lanes = lax.broadcasted_iota(jnp.int32, (16, 128), 1) // 16
    for m in range(4):
        for high in range(2):
            tiles = [back[8 * high + k, :, pl.ds(128 * m, 128)].astype(jnp.float32) for k in range(8)]
            for bit in (1, 2, 4):
                clear = (lanes & bit) == 0
                fresh = list(tiles)
                for k in range(8):
                    if k & bit == 0:
                        a, b = tiles[k], tiles[k | bit]
                        fresh[k] = jnp.where(clear, a, pltpu.roll(b, 16 * bit, 1))
                        fresh[k | bit] = jnp.where(clear, pltpu.roll(a, 128 - 16 * bit, 1), b)
                tiles = fresh
            for k in range(8):
                v, part = 4 * m + k // 2, k % 2
                out_ref[v, :, pl.ds(256 * part + 128 * high, 128)] = tiles[k]

    drain_across(piece, landed, send1, recv1)
    for side in range(2):
        for t in range(1, 4):
            for part in range(2):
                ringed(side, t, part).wait_send()
        ringed(side, 4, side).wait_send()
    for part in range(2):
        for side, t in ((0, 0), (0, 1), (1, 1), (0, 2), (1, 2), (0, 3), (1, 3), (0, 4)):
            shared(side, t, part).wait_send()
    drain_across(outbuf, back, send2, recv2)


def body(projections, ctf_weight, orient, angle_table):
    dma = pltpu.SemaphoreType.DMA
    return pl.pallas_call(
        kernel,
        out_shape=jax.ShapeDtypeStruct((16, 16, 512), jnp.float32),
        in_specs=[pl.BlockSpec(memory_space=pltpu.HBM)] * 4,
        out_specs=pl.BlockSpec(memory_space=pltpu.VMEM),
        scratch_shapes=[
            pltpu.SMEM((4,), jnp.int32),
            pltpu.VMEM((4, 16, 512), jnp.bfloat16),
            pltpu.VMEM((4, 16, 256), jnp.bfloat16),
            pltpu.VMEM((64, 4, 256), jnp.int32),
            dma((4,)),
            pltpu.VMEM((16, 32, 128), jnp.bfloat16),
            pltpu.VMEM((16, 32, 128), jnp.bfloat16),
            pltpu.VMEM((16, 208, 256), jnp.bfloat16),
            pltpu.VMEM((768, 256), jnp.float32),
            pltpu.VMEM((16, 16, 512), jnp.bfloat16),
            pltpu.VMEM((16, 16, 512), jnp.bfloat16),
            dma((16,)), dma((16,)),
            dma((16,)), dma((16,)), dma((16,)), dma((16,)),
            dma((16,)), dma((16,)),
        ],
        compiler_params=pltpu.CompilerParams(
            collective_id=0, has_side_effects=True, vmem_limit_bytes=67043328
        ),
    )(orient, projections, ctf_weight, angle_table)


def solution(mesh):
    placed = (
        P(("rep", "pix"), "slab", None),
        P(("rep", "pix"), "slab", None),
        P(("rep", "pix")),
        P(),
    )
    return jax.shard_map(
        body, mesh=mesh, in_specs=placed, out_specs=P(("rep", "pix"), "slab", None), check_vma=False
    )
```

time: 48.3 us -> 45.8 us (0.948)
  the two profiles are of different devices: /device:TPU:1 before, /device:TPU:96 now
where the time goes in v3:
time: 45.8 us; the launch traced here: 45.5 us
  Pallas kernels  43.6 us (95%)
  local copies, waits for them, and re-layouts  1.88 us (4%)
    pallas_call x1, Pallas kernels, body(): pl.pallas_call(kernel, out_shape=jax.ShapeDtypeStruct((16, 16, 512), jnp....  43.6 us
    unnamed x1, local copies, waits for them, and re-layouts  1.88 us

profile of v3, /device:TPU:96, one launch (start us, length us, event | category | flops | bytes accessed | tf_op | source)
XLA Modules:
  0.0 45.5 jit_solution(8901514809876805584)
XLA Ops:
  0.0 43.6 %shard_map.46 = f32[16,16,512]{2,1,0:T(8,128)} custom-call(s32[4]{0:T(128)} %orient_hbm.1, bf16[4,16,512]{2,1,0:T(8,128)(2,1)} %proj_hbm.1, bf16[4,16,256]{2,1,0:T(8,128)(2,1)} %ctf_hbm.1, s32[64,4,256]{2,1,0:T(4,128)} %table_hbm.1), custom_call_target="tpu_custom_call" | custom-call | tf_op jit(solution)/shard_map/pallas_call | solution.py:338
  43.7 1.9 %copy.6 = f32[16,16,512]{2,1,0:T(8,128)} copy(f32[16,16,512]{2,1,0:T(8,128)} %shard_map.46) | data formatting | bytes 1048576

commit v4 on v3

--- a/solution.py
+++ b/solution.py
@@ -59,7 +59,7 @@
         return carry
 
     lax.fori_loop(1, 16, greet, 0)
-    for peer in (along_z(1), along_z(-1), along_z(2), along_z(-2), partner):
+    for peer in (along_z(1), along_z(-1), partner):
         pl.semaphore_signal(barrier, inc=1, device_id=peer, device_id_type=MESH)
 
     acc[...] = jnp.zeros_like(acc)
@@ -95,7 +95,7 @@
             low_half, second[16 * q : 16 * q + 16], facts
         ).astype(jnp.bfloat16)
 
-    pl.semaphore_wait(barrier, 20)
+    pl.semaphore_wait(barrier, 18)
 
     def across(src, dst, send, recv, k, into):
         to = (me + k) % 16
@@ -158,12 +158,11 @@
         )
 
     def ringed(side, t, part):
-        src = 0 if t < 3 else slot_of(side, 2)
+        src = 0 if t == 1 else slot_of(side, t - 1)
         dst = FAR if t == 4 else slot_of(side, t)
         k = 8 * side + 2 * (t - 1) + part
-        reach = (1, 2, 1, 2)[t - 1]
         return move(
-            src, dst, HALVES[part], send_z.at[k], recv_z.at[k], along_z(reach * (1 - 2 * side))
+            src, dst, HALVES[part], send_z.at[k], recv_z.at[k], along_z(1 - 2 * side)
         )
 
     def shared(side, t, part):
@@ -176,17 +175,17 @@
         k = 2 * k + part
         return move(src, dst, HALVES[part], send_p.at[k], recv_p.at[k], partner)
 
-    def arrive(side, t):
-        for part in range(2):
-            ringed(side, t, part).wait_recv()
-            if t == 2:
-                ringed(side, 3, part).start()
-
-                @pl.when(side == part)
-                def _():
-                    ringed(part, 4, part).start()
-
-            shared(side, t, part).start()
+    def arrive(side, t, part):
+        ringed(side, t, part).wait_recv()
+        if t < 3:
+            ringed(side, t + 1, part).start()
+        elif t == 3:
+
+            @pl.when(side == part)
+            def _():
+                ringed(part, 4, part).start()
+
+        shared(side, t, part).start()
 
     row16 = lax.broadcasted_iota(jnp.int32, (16, 256), 0).astype(jnp.float32)
 
@@ -257,12 +256,10 @@
     near = jnp.where(zpos < 4, 1, 0)
     away = 1 - near
 
-    for t in range(1, 3):
-        for part in range(2):
-            for side in range(2):
-                ringed(side, t, part).start()
-            if t == 1:
-                shared(0, 0, part).start()
+    for part in range(2):
+        for side in range(2):
+            ringed(side, 1, part).start()
+        shared(0, 0, part).start()
 
     def landed_shared(side, t):
         for part in range(2):
@@ -271,22 +268,33 @@
 
     accumulate(0)
     accumulate(landed_shared(0, 0))
-    arrive(near, 1)
+    arrive(near, 1, 0)
+    arrive(near, 1, 1)
     accumulate(slot_of(near, 1))
-    arrive(away, 1)
-    accumulate(landed_shared(near, 1), slot_of(away, 1))
-    arrive(near, 2)
-    accumulate(landed_shared(away, 1), slot_of(near, 2))
-    arrive(away, 2)
-    accumulate(landed_shared(near, 2), slot_of(away, 2))
-    arrive(near, 3)
-    accumulate(landed_shared(away, 2), slot_of(near, 3))
-    arrive(away, 3)
-    for side in range(2):
-        ringed(side, 4, side).wait_recv()
-        shared(0, 4, side).start()
-    accumulate(landed_shared(near, 3), slot_of(away, 3))
-    accumulate(landed_shared(away, 3), FAR)
+    arrive(away, 1, 0)
+    arrive(away, 1, 1)
+    accumulate(slot_of(away, 1))
+    accumulate(landed_shared(near, 1))
+    arrive(near, 2, 0)
+    arrive(away, 2, 0)
+    accumulate(landed_shared(away, 1))
+    arrive(near, 2, 1)
+    arrive(away, 2, 1)
+    accumulate(slot_of(near, 2))
+    accumulate(slot_of(away, 2))
+    arrive(near, 3, 0)
+    accumulate(landed_shared(near, 2))
+    arrive(near, 3, 1)
+    accumulate(slot_of(near, 3))
+    arrive(away, 3, 0)
+    accumulate(landed_shared(away, 2))
+    arrive(away, 3, 1)
+    accumulate(slot_of(away, 3))
+    accumulate(landed_shared(near, 3))
+    arrive(0, 4, 0)
+    accumulate(landed_shared(away, 3))
+    arrive(1, 4, 1)
+    accumulate(FAR)
     accumulate(landed_shared(0, 4))
 
     rows = []

time: 45.8 us -> 44.2 us (0.965)
  Pallas kernels: 43.6 us -> 42.2 us
    pallas_call x1, Pallas kernels: 43.6 us -> 42.2 us  [body(): pl.pallas_call(kernel, out_shape=jax.ShapeDtypeStruct((16, 16, 512), jnp....]
where the time goes in v4:
time: 44.2 us; the launch traced here: 44.1 us
  Pallas kernels  42.2 us (95%)
  local copies, waits for them, and re-layouts  1.88 us (4%)
    pallas_call x1, Pallas kernels, body(): pl.pallas_call(kernel, out_shape=jax.ShapeDtypeStruct((16, 16, 512), jnp....  42.2 us
    unnamed x1, local copies, waits for them, and re-layouts  1.88 us

profile of v4, /device:TPU:96, one launch (start us, length us, event | category | flops | bytes accessed | tf_op | source)
XLA Modules:
  0.0 44.1 jit_solution(11199632959071732921)
XLA Ops:
  0.0 42.2 %shard_map.46 = f32[16,16,512]{2,1,0:T(8,128)} custom-call(s32[4]{0:T(128)} %orient_hbm.1, bf16[4,16,512]{2,1,0:T(8,128)(2,1)} %proj_hbm.1, bf16[4,16,256]{2,1,0:T(8,128)(2,1)} %ctf_hbm.1, s32[64,4,256]{2,1,0:T(4,128)} %table_hbm.1), custom_call_target="tpu_custom_call" | custom-call | tf_op jit(solution)/shard_map/pallas_call | solution.py:346
  42.2 1.9 %copy.6 = f32[16,16,512]{2,1,0:T(8,128)} copy(f32[16,16,512]{2,1,0:T(8,128)} %shard_map.46) | data formatting | bytes 1048576

commit v5 on v4

--- a/solution.py
+++ b/solution.py
@@ -12,17 +12,13 @@
 
 
 def slot_of(side, t):
-    return 2 + 4 * (t - 1) + side
-
-
-def slot_shared(side, t):
-    return 4 + 4 * (t - 1) + side
+    return 2 + 4 * (t - 1) + 2 * side
 
 
 def kernel(
     orient_hbm, proj_hbm, ctf_hbm, table_hbm, out_ref,
     orient_ref, proj_ref, ctf_ref, table_ref, stage, piece, landed, gath, acc, outbuf, back,
-    send1, recv1, send_z, recv_z, send_p, recv_p, send2, recv2,
+    send1, recv1, send_z, recv_z, send_p, send_o, recv_o, send2, recv2,
 ):
     staged = [
         pltpu.make_async_copy(src, dst, stage.at[k])
@@ -40,6 +36,8 @@
     zpos = pix * 4 + zl
     me = xc * 4 + yc
     sub = core * 2 + pix
+    hub = core == 1
+    mine = 1 - core
 
     def plane(q):
         return ((q // 4) * 2 + core, (q % 4) * 4 + zl, pix)
@@ -138,10 +136,10 @@
         bottom = jnp.where(half, pltpu.roll(a, 64, 1), b)
         at = pl.ds(128 * (j % 2), 128)
         row = 16 + 48 * (j // 2)
-        gath[0, row : row + 32, at] = top
-        gath[0, row + 32 : row + 48, at] = bottom[0:16].astype(jnp.bfloat16)
+        gath[mine, row : row + 32, at] = top
+        gath[mine, row + 32 : row + 48, at] = bottom[0:16].astype(jnp.bfloat16)
         tables.append(bottom[16:20])
-    gath[0, 0:16, :] = jnp.concatenate(
+    gath[mine, 0:16, :] = jnp.concatenate(
         [
             jnp.concatenate([tables[2 * g][f : f + 1], tables[2 * g + 1][f : f + 1]], axis=1)
             for f in range(4)
@@ -157,35 +155,49 @@
             send_sem=send, recv_sem=recv, device_id=to, device_id_type=MESH,
         )
 
+    def slots(side, t, part):
+        return (FAR if t == 4 else slot_of(side, t)) + part // 2
+
+    def index(side, t, part):
+        return 16 * side + 4 * (t - 1) + part
+
     def ringed(side, t, part):
-        src = 0 if t == 1 else slot_of(side, t - 1)
-        dst = FAR if t == 4 else slot_of(side, t)
-        k = 8 * side + 2 * (t - 1) + part
+        src = part // 2 if t == 1 else slot_of(side, t - 1) + part // 2
+        k = index(side, t, part)
         return move(
-            src, dst, HALVES[part], send_z.at[k], recv_z.at[k], along_z(1 - 2 * side)
+            src, slots(side, t, part), HALVES[part % 2], send_z.at[k], recv_z.at[k],
+            along_z(1 - 2 * side),
         )
 
     def shared(side, t, part):
-        if t == 0:
-            src, dst, k = 0, 1, 0
-        elif t == 4:
-            src, dst, k = FAR, FAR + 1, 7
-        else:
-            src, dst, k = slot_of(side, t), slot_shared(side, t), 2 * t - 1 + side
-        k = 2 * k + part
-        return move(src, dst, HALVES[part], send_p.at[k], recv_p.at[k], partner)
+        slot, k = slots(side, t, part), index(side, t, part)
+        return move(slot, slot, HALVES[part % 2], send_p.at[k], recv_z.at[k], partner)
+
+    def exchanged(part):
+        return move(mine, mine, HALVES[part], send_o.at[part], recv_o.at[part], partner)
+
+    def arrive_partner(part):
+        exchanged(part).wait_recv()
+
+        @pl.when(hub)
+        def _():
+            for side in range(2):
+                ringed(side, 1, 2 + part).start()
 
     def arrive(side, t, part):
         ringed(side, t, part).wait_recv()
-        if t < 3:
-            ringed(side, t + 1, part).start()
-        elif t == 3:
-
-            @pl.when(side == part)
+
+        @pl.when(hub)
+        def _():
+            if t < 3:
+                ringed(side, t + 1, part).start()
+            shared(side, t, part).start()
+
+        if t == 3:
+
+            @pl.when(hub & (side == part % 2))
             def _():
-                ringed(part, 4, part).start()
-
-        shared(side, t, part).start()
+                ringed(part % 2, 4, part).start()
 
     row16 = lax.broadcasted_iota(jnp.int32, (16, 256), 0).astype(jnp.float32)
 
@@ -256,46 +268,60 @@
     near = jnp.where(zpos < 4, 1, 0)
     away = 1 - near
 
+    @pl.when(hub)
+    def _():
+        for part in range(2):
+            for side in range(2):
+                ringed(side, 1, part).start()
+
     for part in range(2):
-        for side in range(2):
-            ringed(side, 1, part).start()
-        shared(0, 0, part).start()
-
-    def landed_shared(side, t):
-        for part in range(2):
-            shared(side, t, part).wait_recv()
-        return {0: 1, 4: FAR + 1}[t] if t in (0, 4) else slot_shared(side, t)
-
-    accumulate(0)
-    accumulate(landed_shared(0, 0))
+        exchanged(part).start()
+    accumulate(mine)
+    arrive_partner(0)
+    arrive_partner(1)
+    accumulate(core)
     arrive(near, 1, 0)
     arrive(near, 1, 1)
     accumulate(slot_of(near, 1))
+    arrive(near, 1, 2)
+    arrive(near, 1, 3)
+    accumulate(slot_of(near, 1) + 1)
     arrive(away, 1, 0)
     arrive(away, 1, 1)
     accumulate(slot_of(away, 1))
-    accumulate(landed_shared(near, 1))
+    arrive(away, 1, 2)
+    arrive(away, 1, 3)
+    accumulate(slot_of(away, 1) + 1)
     arrive(near, 2, 0)
     arrive(away, 2, 0)
-    accumulate(landed_shared(away, 1))
     arrive(near, 2, 1)
     arrive(away, 2, 1)
     accumulate(slot_of(near, 2))
+    arrive(near, 2, 2)
+    arrive(away, 2, 2)
     accumulate(slot_of(away, 2))
+    arrive(near, 2, 3)
+    arrive(away, 2, 3)
     arrive(near, 3, 0)
-    accumulate(landed_shared(near, 2))
+    accumulate(slot_of(near, 2) + 1)
     arrive(near, 3, 1)
+    accumulate(slot_of(away, 2) + 1)
+    arrive(near, 3, 2)
     accumulate(slot_of(near, 3))
     arrive(away, 3, 0)
-    accumulate(landed_shared(away, 2))
+    arrive(near, 3, 3)
     arrive(away, 3, 1)
+    accumulate(slot_of(near, 3) + 1)
+    arrive(away, 3, 2)
+    arrive(away, 3, 3)
     accumulate(slot_of(away, 3))
-    accumulate(landed_shared(near, 3))
+    accumulate(slot_of(away, 3) + 1)
     arrive(0, 4, 0)
-    accumulate(landed_shared(away, 3))
     arrive(1, 4, 1)
     accumulate(FAR)
-    accumulate(landed_shared(0, 4))
+    arrive(0, 4, 2)
+    arrive(1, 4, 3)
+    accumulate(FAR + 1)
 
     rows = []
     for v in range(16):
@@ -327,17 +353,20 @@
                 tiles = fresh
             for k in range(8):
                 v, part = 4 * m + k // 2, k % 2
-                out_ref[v, :, pl.ds(256 * part + 128 * high, 128)] = tiles[k]
+                out_ref[v, :, pl.ds(256 * part + 128 * high, 128)] = tiles[k].astype(jnp.bfloat16)
 
     drain_across(piece, landed, send1, recv1)
-    for side in range(2):
-        for t in range(1, 4):
-            for part in range(2):
-                ringed(side, t, part).wait_send()
-        ringed(side, 4, side).wait_send()
     for part in range(2):
-        for side, t in ((0, 0), (0, 1), (1, 1), (0, 2), (1, 2), (0, 3), (1, 3), (0, 4)):
-            shared(side, t, part).wait_send()
+        exchanged(part).wait_send()
+
+    @pl.when(hub)
+    def _():
+        for side in range(2):
+            for t in range(1, 5):
+                for part in range(4) if t < 4 else (side, 2 + side):
+                    ringed(side, t, part).wait_send()
+                    shared(side, t, part).wait_send()
+
     drain_across(outbuf, back, send2, recv2)
 
 
@@ -345,7 +374,7 @@
     dma = pltpu.SemaphoreType.DMA
     return pl.pallas_call(
         kernel,
-        out_shape=jax.ShapeDtypeStruct((16, 16, 512), jnp.float32),
+        out_shape=jax.ShapeDtypeStruct((16, 16, 512), jnp.bfloat16),
         in_specs=[pl.BlockSpec(memory_space=pltpu.HBM)] * 4,
         out_specs=pl.BlockSpec(memory_space=pltpu.VMEM),
         scratch_shapes=[
@@ -361,13 +390,13 @@
             pltpu.VMEM((16, 16, 512), jnp.bfloat16),
             pltpu.VMEM((16, 16, 512), jnp.bfloat16),
             dma((16,)), dma((16,)),
-            dma((16,)), dma((16,)), dma((16,)), dma((16,)),
+            dma((32,)), dma((32,)), dma((32,)), dma((2,)), dma((2,)),
             dma((16,)), dma((16,)),
         ],
         compiler_params=pltpu.CompilerParams(
             collective_id=0, has_side_effects=True, vmem_limit_bytes=67043328
         ),
-    )(orient, projections, ctf_weight, angle_table)
+    )(orient, projections, ctf_weight, angle_table).astype(jnp.float32)
 
 
 def solution(mesh):

time: 44.2 us -> 42.9 us (0.971)
  local copies, waits for them, and re-layouts: 1.88 us -> 0 us
  other arithmetic: 0 us -> 1.8 us
  Pallas kernels: 42.2 us -> 40.9 us
    unnamed x1 -> x0, local copies, waits for them, and re-layouts: 1.88 us -> none
    convert_element_type x0 -> x1, other arithmetic: none -> 1.8 us  [body(): return pl.pallas_call(kernel, out_shape=jax.ShapeDtypeStruct((16, 16, 512...]
    pallas_call x1, Pallas kernels: 42.2 us -> 40.9 us  [body(): pl.pallas_call(kernel, out_shape=jax.ShapeDtypeStruct((16, 16, 512), jnp....]
where the time goes in v5:
time: 42.9 us; the launch traced here: 42.7 us
  Pallas kernels  40.9 us (95%)
  other arithmetic  1.8 us (4%)
    pallas_call x1, Pallas kernels, body(): pl.pallas_call(kernel, out_shape=jax.ShapeDtypeStruct((16, 16, 512), jnp....  40.9 us
    convert_element_type x1, other arithmetic, body(): return pl.pallas_call(kernel, out_shape=jax.ShapeDtypeStruct((16, 16, 512...  1.8 us

profile of v5, /device:TPU:96, one launch (start us, length us, event | category | flops | bytes accessed | tf_op | source)
XLA Modules:
  0.0 42.7 jit_solution(451107657939740776)
XLA Ops:
  0.0 40.9 %shard_map.46 = bf16[16,16,512]{2,1,0:T(8,128)(2,1)} custom-call(s32[4]{0:T(128)} %orient_hbm.1, bf16[4,16,512]{2,1,0:T(8,128)(2,1)} %proj_hbm.1, bf16[4,16,256]{2,1,0:T(8,128)(2,1)} %ctf_hbm.1, s32[64,4,256]{2,1,0:T(4,128)} %table_hbm.1), custom_call_target="tpu_custom_call" | custom-call | tf_op jit(solution)/shard_map/pallas_call | solution.py:375
  40.9 1.8 %convert_element_type.3 = f32[16,16,512]{2,1,0:T(8,128)} convert(bf16[16,16,512]{2,1,0:T(8,128)(2,1)} %shard_map.46) | non-fusion elementwise | flops 131072 | bytes 786432 | tf_op jit(solution)/shard_map/convert_element_type | solution.py:399

commit v6 on v5

--- a/solution.py
+++ b/solution.py
@@ -8,6 +8,10 @@
 MESH = pl.DeviceIdType.MESH
 RING = 8
 FAR = 14
+FARTHEST_FIRST = (
+    (2, 2), (2, 1), (2, 3), (1, 2), (3, 2), (1, 1), (1, 3), (3, 1), (3, 3),
+    (2, 0), (0, 2), (1, 0), (3, 0), (0, 1), (0, 3),
+)
 HALVES = ((0, 112), (112, 96))
 
 
@@ -102,12 +106,13 @@
             device_id=plane(to), device_id_type=MESH,
         )
 
-    def start_across(*refs):
-        def go(k, carry):
-            across(*refs, k, me).start()
-            return carry
-
-        lax.fori_loop(1, 16, go, 0)
+    def start_across(src, dst, send, recv):
+        for dx, dy in FARTHEST_FIRST:
+            to = (xc + dx) % 4 * 4 + (yc + dy) % 4
+            pltpu.make_async_remote_copy(
+                src_ref=src.at[to], dst_ref=dst.at[me], send_sem=send.at[to], recv_sem=recv.at[me],
+                device_id=plane(to), device_id_type=MESH,
+            ).start()
 
     def land_across(*refs):
         def go(k, carry):

time: 42.9 us -> 42.3 us (0.986)
  Pallas kernels: 40.9 us -> 40.3 us
    pallas_call x1, Pallas kernels: 40.9 us -> 40.3 us  [body(): pl.pallas_call(kernel, out_shape=jax.ShapeDtypeStruct((16, 16, 512), jnp....]
where the time goes in v6:
time: 42.3 us; the launch traced here: 42.2 us
  Pallas kernels  40.3 us (95%)
  other arithmetic  1.8 us (4%)
    pallas_call x1, Pallas kernels, body(): pl.pallas_call(kernel, out_shape=jax.ShapeDtypeStruct((16, 16, 512), jnp....  40.3 us
    convert_element_type x1, other arithmetic, body(): return pl.pallas_call(kernel, out_shape=jax.ShapeDtypeStruct((16, 16, 512...  1.8 us

profile of v6, /device:TPU:96, one launch (start us, length us, event | category | flops | bytes accessed | tf_op | source)
XLA Modules:
  0.0 42.2 jit_solution(14036769612292018070)
XLA Ops:
  0.0 40.3 %shard_map.46 = bf16[16,16,512]{2,1,0:T(8,128)(2,1)} custom-call(s32[4]{0:T(128)} %orient_hbm.1, bf16[4,16,512]{2,1,0:T(8,128)(2,1)} %proj_hbm.1, bf16[4,16,256]{2,1,0:T(8,128)(2,1)} %ctf_hbm.1, s32[64,4,256]{2,1,0:T(4,128)} %table_hbm.1), custom_call_target="tpu_custom_call" | custom-call | tf_op jit(solution)/shard_map/pallas_call | solution.py:380
  40.4 1.8 %convert_element_type.3 = f32[16,16,512]{2,1,0:T(8,128)} convert(bf16[16,16,512]{2,1,0:T(8,128)(2,1)} %shard_map.46) | non-fusion elementwise | flops 131072 | bytes 786432 | tf_op jit(solution)/shard_map/convert_element_type | solution.py:404

commit v7 on v6

--- a/solution.py
+++ b/solution.py
@@ -61,8 +61,13 @@
         return carry
 
     lax.fori_loop(1, 16, greet, 0)
-    for peer in (along_z(1), along_z(-1), partner):
-        pl.semaphore_signal(barrier, inc=1, device_id=peer, device_id_type=MESH)
+    pl.semaphore_signal(barrier, inc=1, device_id=partner, device_id_type=MESH)
+
+    @pl.when(hub)
+    def _():
+        for peer in (along_z(1), along_z(-1)):
+            pl.semaphore_signal(barrier, inc=1, device_id=peer, device_id_type=MESH)
+
 
     acc[...] = jnp.zeros_like(acc)
     for copy in staged:
@@ -97,7 +102,7 @@
             low_half, second[16 * q : 16 * q + 16], facts
         ).astype(jnp.bfloat16)
 
-    pl.semaphore_wait(barrier, 18)
+    pl.semaphore_wait(barrier, 16 + 2 * core)
 
     def across(src, dst, send, recv, k, into):
         to = (me + k) % 16

time: 42.3 us -> 42.3 us (level)
  no operation moved by 1% of the time
where the time goes in v7:
time: 42.3 us; the launch traced here: 42.1 us
  Pallas kernels  40.3 us (95%)
  other arithmetic  1.8 us (4%)
    pallas_call x1, Pallas kernels, body(): pl.pallas_call(kernel, out_shape=jax.ShapeDtypeStruct((16, 16, 512), jnp....  40.3 us
    convert_element_type x1, other arithmetic, body(): return pl.pallas_call(kernel, out_shape=jax.ShapeDtypeStruct((16, 16, 512...  1.8 us

profile of v7, /device:TPU:96, one launch (start us, length us, event | category | flops | bytes accessed | tf_op | source)
XLA Modules:
  0.0 42.1 jit_solution(237264408987918206)
XLA Ops:
  0.0 40.3 %shard_map.46 = bf16[16,16,512]{2,1,0:T(8,128)(2,1)} custom-call(s32[4]{0:T(128)} %orient_hbm.1, bf16[4,16,512]{2,1,0:T(8,128)(2,1)} %proj_hbm.1, bf16[4,16,256]{2,1,0:T(8,128)(2,1)} %ctf_hbm.1, s32[64,4,256]{2,1,0:T(4,128)} %table_hbm.1), custom_call_target="tpu_custom_call" | custom-call | tf_op jit(solution)/shard_map/pallas_call | solution.py:385
  40.3 1.8 %convert_element_type.3 = f32[16,16,512]{2,1,0:T(8,128)} convert(bf16[16,16,512]{2,1,0:T(8,128)(2,1)} %shard_map.46) | non-fusion elementwise | flops 131072 | bytes 786432 | tf_op jit(solution)/shard_map/convert_element_type | solution.py:409
